TPU v7x, 32 devices: a whole 2x2x4 slice. The times are simulated.
32 devices in a mesh: region: 8 (over z, x), tm: 4 (over y, core).
Axes of the slice: x: 2, y: 2, z: 4, core: 2. Of those that a mesh axis runs over, the one named last changes fastest.
Arguments:
- observations: bfloat16 [8, 4, 2048, 512], P('region', 'tm'), may hold values from -160 to 160
- counts: int32 [8, 4], P('region', 'tm'), may hold values from 1 to 8, as said below
- visible: int32 [8, 8], replicated, may hold values 0 or 1
- latents: bfloat16 [8, 32, 512], P('region'), may hold values from -6 to 6
- lat_gain: float32 [512], replicated, may hold values from 0.5 to 1.5
- mlp_gain: float32 [512], replicated, may hold values from 0.5 to 1.5
- w_query: bfloat16 [512, 512], replicated, may hold values from -0.25 to 0.25
- w_keyval: bfloat16 [512, 1024], replicated, may hold values from -0.25 to 0.25
- w_out: bfloat16 [512, 512], replicated, may hold values from -0.25 to 0.25
- w_up: bfloat16 [512, 2048], P(None, 'tm'), may hold values from -0.25 to 0.25
- w_down: bfloat16 [2048, 512], P('tm'), may hold values from -0.125 to 0.125
Outputs:
- encoded: bfloat16 [8, 32, 512], P('region')
Inputs may be any that keep to these rules, and one draw needn't show every extreme that they name: `counts`: some region and time slot holds 8 blocks.
All inputs are finite; a program needn't handle non-finite values.
Results may differ from a plain program's by a relative error of at most 0.0055.
The roundings to bfloat16 on the way count: a program that leaves them out, or rounds other values in their place, can miss the bound.
Values may be sent and summed in bfloat16 or wider, within the bound.
A program may use at most 64 MiB of HBM per device.

v0:
```python
import math

import jax
import jax.numpy as jnp
from jax import lax
from jax.sharding import PartitionSpec as P

H = 8
BLK = 256


NEG = -1e30


def joined(x, axis, combine):
    everything = jax.tree.map(lambda part: lax.all_gather(part, axis), x)
    leading = jax.tree.map(lambda part: part[0], everything)

    def step(k, so_far):
        return combine(so_far, jax.tree.map(lambda part: part[k], everything))

    return lax.fori_loop(1, lax.axis_size(axis), step, leading)


def layer_norm(values, gain):
    average = jnp.mean(values, axis=-1, keepdims=True)
    centered = values - average
    variance = jnp.mean(centered * centered, axis=-1, keepdims=True)
    return centered * lax.rsqrt(variance + 1e-05) * gain


def expand(factor, model_width):
    return jnp.repeat(factor, model_width // factor.shape[-1], axis=-1)


def combine(first, second):
    first_num, first_den, first_peak = first
    second_num, second_den, second_peak = second
    highest = jnp.maximum(first_peak, second_peak)
    first_scale = jnp.exp(first_peak - highest)
    second_scale = jnp.exp(second_peak - highest)
    numerator = first_num * expand(first_scale, first_num.shape[-1]) + second_num * expand(
        second_scale, second_num.shape[-1]
    )
    return (numerator, first_den * first_scale + second_den * second_scale, highest)


def partials(query_rows, key_heads, value_heads, allowed, head_size):
    row_count = query_rows.shape[0]
    query_heads = query_rows.reshape(row_count, H, head_size)
    scores = jnp.einsum(
        "qhd,khd->hqk", query_heads, key_heads, preferred_element_type=jnp.float32
    ) * head_size ** (-0.5)
    scores = jnp.where(allowed[None], scores, NEG)
    peaks = jnp.max(scores, axis=-1)
    weights = jnp.where(allowed[None], jnp.exp(scores - peaks[..., None]), 0.0)
    denominator = jnp.sum(weights, axis=-1)
    numerator = jnp.einsum(
        "hqk,khd->qhd",
        weights.astype(jnp.bfloat16),
        value_heads,
        preferred_element_type=jnp.float32,
    )
    return (numerator.reshape(row_count, H * head_size), denominator.T, peaks.T)


def on_device(
    observations,
    counts,
    visible,
    latents,
    lat_gain,
    mlp_gain,
    w_query,
    w_keyval,
    w_out,
    w_up,
    w_down,
):
    regions = lax.axis_size("region")
    own_region = lax.axis_index("region")
    latent_rows = latents.shape[1]
    model_width = latents.shape[2]
    head_size = model_width // H
    observed = observations[0, 0]
    obs_rows = observed.shape[0]
    latent_state = latents[0].astype(jnp.float32)
    normed = layer_norm(latent_state, lat_gain).astype(jnp.bfloat16)
    own_queries = jnp.dot(normed, w_query, preferred_element_type=jnp.float32).astype(jnp.bfloat16)
    every_query = lax.all_gather(own_queries, "region", axis=0, tiled=True)
    keyval = jnp.dot(observed, w_keyval, preferred_element_type=jnp.float32).astype(jnp.bfloat16)
    key_heads = keyval[:, :model_width].reshape(obs_rows, H, head_size)
    value_heads = keyval[:, model_width:].reshape(obs_rows, H, head_size)
    live_rows = lax.iota(jnp.int32, obs_rows) < counts[0, 0] * BLK
    column = lax.dynamic_slice_in_dim(visible, own_region, 1, 1)[:, 0]
    sees_source = (column > 0) | (lax.iota(jnp.int32, regions) == own_region)
    per_block = math.gcd(regions, max(1, 256 // latent_rows))
    block_count = regions // per_block
    query_blocks = every_query.reshape(block_count, per_block * latent_rows, model_width)
    sees_blocks = jnp.repeat(sees_source, latent_rows).reshape(block_count, per_block * latent_rows)

    def one_block(operands):
        query_rows, sees_rows = operands
        allowed = sees_rows[:, None] & live_rows[None, :]
        return partials(query_rows, key_heads, value_heads, allowed, head_size)

    numerators, denominators, peaks = lax.map(one_block, (query_blocks, sees_blocks))
    numerators = numerators.reshape(regions, latent_rows, model_width)
    denominators = denominators.reshape(regions, latent_rows, H)
    peaks = peaks.reshape(regions, latent_rows, H)
    got_num, got_den, got_peak = (
        lax.all_to_all(numerators, "region", split_axis=0, concat_axis=0, tiled=True),
        lax.all_to_all(denominators, "region", split_axis=0, concat_axis=0, tiled=True),
        lax.all_to_all(peaks, "region", split_axis=0, concat_axis=0, tiled=True),
    )
    highest = jnp.max(got_peak, axis=0)
    factor = jnp.exp(got_peak - highest[None])
    numerator = jnp.sum(got_num * expand(factor, model_width), axis=0)
    denominator = jnp.sum(got_den * factor, axis=0)
    numerator, denominator, highest = joined((numerator, denominator, highest), "tm", combine)
    attended = (numerator / expand(denominator, model_width)).astype(jnp.bfloat16)
    residual = latent_state + jnp.dot(attended, w_out, preferred_element_type=jnp.float32)
    normed2 = layer_norm(residual, mlp_gain).astype(jnp.bfloat16)
    hidden = jax.nn.gelu(
        jnp.dot(normed2, w_up, preferred_element_type=jnp.float32), approximate=True
    ).astype(jnp.bfloat16)
    mlp_part = jnp.dot(hidden, w_down, preferred_element_type=jnp.float32)
    mlp_total = lax.psum(mlp_part, "tm")
    return (residual + mlp_total).astype(jnp.bfloat16)[None]


def solution(mesh):
    placed = (
        P("region", "tm", None, None),
        P("region", "tm"),
        P(),
        P("region", None, None),
        P(),
        P(),
        P(),
        P(),
        P(),
        P(None, "tm"),
        P("tm", None),
    )
    return jax.shard_map(
        on_device, mesh=mesh, in_specs=placed, out_specs=P("region", None, None), check_vma=False
    )
```

profile of v0, /device:TPU:0, one launch (start us, length us, event | category | flops | bytes accessed | tf_op | source)
XLA Modules:
  0.0 166.7 jit_solution(793247751511443457)
XLA Ops:
  6.5 1.0 fusion.44
  7.6 0.1 broadcast_in_dim.82
  7.6 0.1 and.27
  8.4 0.9 convert_reduce_fusion
  9.3 0.9 fusion.16
  10.2 1.3 convolution_convert_fusion.1
  11.5 32.6 %all_gather.19 = bf16[256,512]{1,0:T(8,128)(2,1)S(1)} all-gather(bf16[32,512]{1,0:T(8,128)(2,1)S(1)} %convolution_convert_fusion.1), channel_id=1, replica_groups=mesh['region'=8,'tm'=4] {'region'}, dimensions={0}, use_global_device_ids=true | all-gather | bytes 294912 | tf_op jit(solution)/shard_map/all_gather | solution.py:90
  44.1 0.1 copy.27
  44.3 3.6 %convolution_convert_fusion = bf16[2048,1024]{0,1:T(8,128)(2,1)S(1)} fusion(bf16[512,1024]{1,0:T(8,128)(2,1)} %param.20, bf16[1,1,2048,512]{3,2,1,0:T(8,128)(2,1)S(1)} %copy-done), kind=kOutput, calls=%fused_computation.17 | convolution fusion | flops 2149580800 | bytes 7340032 | tf_op jit(solution)/shard_map/dot_general | solution.py:91
  47.9 1.8 %fusion.53 = (bf16[2048,512]{0,1:T(8,128)(2,1)S(1)}, bf16[2048,512]{0,1:T(8,128)(2,1)}) fusion(bf16[2048,1024]{0,1:T(8,128)(2,1)S(1)} %convolution_convert_fusion), kind=kLoop, calls=%fused_computation.77 | loop fusion | bytes 8388608 | tf_op jit(solution)/shard_map/slice | solution.py:92
  49.7 0.3 broadcast_and_fusion
  50.0 3.2 %fusion.3 = (f32[8,256]{1,0:T(8,128)S(1)}, f32[8,256,2048]{2,1,0:T(8,128)S(1)}) fusion(pred[256,2048]{1,0:T(8,128)(4,1)S(1)} %broadcast_and_fusion, bf16[256,8,64]{0,2,1:T(8,128)(2,1)S(1)} %bitcast.84, bf16[2048,8,64]{0,2,1:T(8,128)(2,1)S(1)} %bitcast.81), kind=kOutput, calls=%fused_computation.12 | convolution fusion | flops 549451776 | bytes 19668992 | tf_op jit(solution)/shard_map/while/body/eval_jaxpr/qhd,khd->hqk/dot_general | solution.py:51
  53.2 5.7 %copy-done.1 = f32[8,256,2048]{2,1,0:T(8,128)} copy-done((f32[8,256,2048]{2,1,0:T(8,128)}, f32[8,256,2048]{2,1,0:T(8,128)S(1)}, u32[]{:S(2)}) %copy-start.1) | copy-done | bytes 16777240
  58.9 5.0 %fusion.4 = f32[8,256]{1,0:T(8,128)S(1)} fusion(f32[8,256,2048]{2,1,0:T(8,128)S(1)} %get-tuple-element.250, f32[8,256]{1,0:T(8,128)S(1)} %get-tuple-element.249, pred[256,2048]{1,0:T(8,128)(4,1)S(1)} %broadcast_and_fusion), kind=kLoop, calls=%fused_computation.13 | loop fusion | flops 20969472 | bytes 17317888 | tf_op jit(solution)/shard_map/while/body/eval_jaxpr/reduce_sum | solution.py:57
  63.9 0.1 reshape.129
  63.9 0.7 reshape.151
  64.6 5.5 %all-to-all-start.2 = ((f32[8,1,256]{2,1,0:T(1,128)}), f32[8,1,256]{2,1,0:T(1,128)S(1)}, u32[]{:S(2)}, u32[]{:S(2)}) async-start(f32[8,1,256]{2,1,0:T(1,128)} %reshape.151), calls=%async_computation.2 | async-start | bytes 16384 | tf_op jit(solution)/shard_map/all_to_all | solution.py:113
  70.2 0.7 reshape.149
  70.9 5.8 %all-to-all-done.2 = f32[8,1,256]{2,1,0:T(1,128)S(1)} async-done(((f32[8,1,256]{2,1,0:T(1,128)}), f32[8,1,256]{2,1,0:T(1,128)S(1)}, u32[]{:S(2)}, u32[]{:S(2)}) %all-to-all-start.2) | async-done | bytes 8224 | tf_op jit(solution)/shard_map/all_to_all | solution.py:113
  76.7 3.3 %all-to-all-start.1 = ((f32[8,1,256]{2,1,0:T(1,128)}), f32[8,1,256]{2,1,0:T(1,128)S(1)}, u32[]{:S(2)}, u32[]{:S(2)}) async-start(f32[8,1,256]{2,1,0:T(1,128)} %reshape.149), calls=%async_computation.1 | async-start | bytes 16384 | tf_op jit(solution)/shard_map/all_to_all | solution.py:114
  80.0 9.4 %fusion.10 = f32[256,8,64]{0,2,1:T(8,128)} fusion(bf16[2048,8,64]{0,2,1:T(8,128)(2,1)} %bitcast.82, f32[8,256,2048]{2,1,0:T(8,128)} %copy-done.1, f32[8,256]{1,0:T(8,128)S(1)} %get-tuple-element.249, pred[256,2048]{1,0:T(8,128)(4,1)S(1)} %broadcast_and_fusion), kind=kOutput, calls=%fused_computation.19 | convolution fusion | flops 557842432 | bytes 19931136 | tf_op jit(solution)/shard_map/while/body/eval_jaxpr/hqk,khd->qhd/dot_general | solution.py:58
  89.4 1.5 copy.28
  90.9 1.1 reshape.126
  92.0 5.9 %all-to-all-start = ((f32[8,32,512]{2,1,0:T(8,128)}), f32[8,32,512]{2,1,0:T(8,128)}, u32[]{:S(2)}, u32[]{:S(2)}) async-start(f32[8,32,512]{2,1,0:T(8,128)} %reshape.126), calls=%async_computation | async-start | bytes 1048576 | tf_op jit(solution)/shard_map/all_to_all | solution.py:112
  98.0 0.6 broadcast.93
  98.5 0.7 reduce.4
  99.3 0.1 reshape.152
  99.3 0.7 reduce.3
  100.1 0.1 reshape.150
  100.2 0.1 copy.31
  100.3 0.3 broadcast_in_dim.86
  100.6 1.1 reshape.128
  101.7 5.2 %all-gather.3 = f32[4,32,8]{1,2,0:T(8,128)S(1)} all-gather(f32[1,32,8]{1,2,0:T(8,128)S(1)} %bitcast.90), channel_id=3, replica_groups=mesh['region'=8,'tm'=4] {'tm'}, dimensions={0}, use_global_device_ids=true | all-gather | bytes 5120 | tf_op jit(solution)/shard_map/all_gather | solution.py:16
  106.9 0.1 copy.34
  107.0 5.2 %all-gather.4 = f32[4,32,8]{1,2,0:T(8,128)S(1)} all-gather(f32[1,32,8]{1,2,0:T(8,128)S(1)} %bitcast.88), channel_id=4, replica_groups=mesh['region'=8,'tm'=4] {'tm'}, dimensions={0}, use_global_device_ids=true | all-gather | bytes 5120 | tf_op jit(solution)/shard_map/all_gather | solution.py:16
  112.2 0.1 copy.35
  112.2 1.3 multiply_reduce_fusion
  113.5 5.8 %all-gather = f32[128,512]{1,0:T(8,128)S(1)} all-gather(f32[32,512]{1,0:T(8,128)S(1)} %multiply_reduce_fusion), channel_id=2, replica_groups=mesh['region'=8,'tm'=4] {'tm'}, dimensions={0}, use_global_device_ids=true | all-gather | bytes 327680 | tf_op jit(solution)/shard_map/all_gather | solution.py:16
  119.4 1.9 %while.12 = (s32[]{:T(128)}, f32[32,512]{1,0:T(8,128)S(1)}, f32[32,8]{1,0:T(8,128)S(1)}, f32[32,8]{1,0:T(8,128)S(1)}, f32[4,32,8]{1,2,0:T(8,128)S(1)}, /*index=5...) while((s32[]{:T(128)}, f32[32,512]{1,0:T(8,128)S(1)}, ...), condition=%wide.region_8.9_spmd, body=%wide.region_7.8_spmd.sunk | while | flops 50693 | bytes 739479 | solution.py:22
  119.4 0.1 copy.48
  119.5 0.1 copy.49
  119.6 0.1 broadcast_in_dim.111
  119.7 0.1 reshape.155
  119.8 0.1 broadcast_in_dim.112
  119.9 0.1 reshape.156
  120.0 0.1 copy.48
  120.1 0.1 copy.49
  120.2 0.1 broadcast_in_dim.111
  120.3 0.1 reshape.155
  120.4 0.1 broadcast_in_dim.112
  120.5 0.1 reshape.156
  120.7 0.1 copy.48
  120.7 0.1 copy.49
  120.8 0.1 broadcast_in_dim.111
  120.9 0.1 reshape.155
  121.0 0.1 broadcast_in_dim.112
  121.1 0.1 reshape.156
  121.3 0.1 broadcast_in_dim.88
  121.4 0.1 reshape.130
  121.5 1.3 fusion.54
  122.8 0.2 multiply_reduce_fusion.1
  123.0 2.2 %fusion.28 = f32[32,512]{1,0:T(8,128)} fusion(bf16[512,512]{1,0:T(8,128)(2,1)} %param.23, bf16[512,512]{1,0:T(8,128)(2,1)} %param.22, f32[32,512]{1,0:T(8,128)S(1)} %get-tuple-element.252, f32[512]{0:T(512)S(1)} %copy-done.3, f32[32]{0:T(128)S(1)} %add_rsqrt_fusion, f32[32]{0:T(128)S(1)} %broadcast_multiply_fusion), kind=kOutput, calls=%fused_computation.46 | convolution fusion | flops 33767424 | bytes 1181952 | tf_op jit(solution)/shard_map/dot_general | solution.py:127
  125.3 33.1 %all-reduce.2.cloned.1.call-done = f32[32,512]{1,0:T(8,128)} async-done(((f32[32,512]{1,0:T(8,128)}), f32[32,512]{1,0:T(8,128)}) %all-reduce.2.cloned.1.call-update) | async-done | bytes 65552 | tf_op jit(solution)/shard_map/psum | solution.py:128
  158.4 1.5 fusion.29
  (34 shorter events, 0.4 us)
Async XLA Ops:
  6.5 37.7 %copy-start = (bf16[1,1,2048,512]{3,2,1,0:T(8,128)(2,1)S(1)}, bf16[1,1,2048,512]{3,2,1,0:T(8,128)(2,1)}, u32[]{:S(2)}) copy-start(bf16[1,1,2048,512]{3,2,1,0:T(8,128)(2,1)} %param.13) | copy-start | bytes 6291460
  53.2 5.7 %copy-start.1 = (f32[8,256,2048]{2,1,0:T(8,128)}, f32[8,256,2048]{2,1,0:T(8,128)S(1)}, u32[]{:S(2)}) copy-start(f32[8,256,2048]{2,1,0:T(8,128)S(1)} %get-tuple-element.250) | copy-start | bytes 50331652
  64.6 12.0 %all-to-all-start.2 = ((f32[8,1,256]{2,1,0:T(1,128)}), f32[8,1,256]{2,1,0:T(1,128)S(1)}, u32[]{:S(2)}, u32[]{:S(2)}) async-start(f32[8,1,256]{2,1,0:T(1,128)} %reshape.151), calls=%async_computation.2 | async-start | bytes 16384 | tf_op jit(solution)/shard_map/all_to_all | solution.py:113
  76.7 15.3 %all-to-all-start.1 = ((f32[8,1,256]{2,1,0:T(1,128)}), f32[8,1,256]{2,1,0:T(1,128)S(1)}, u32[]{:S(2)}, u32[]{:S(2)}) async-start(f32[8,1,256]{2,1,0:T(1,128)} %reshape.149), calls=%async_computation.1 | async-start | bytes 16384 | tf_op jit(solution)/shard_map/all_to_all | solution.py:114
  80.0 41.5 %copy-start.2 = (bf16[1,32,512]{2,1,0:T(8,128)(2,1)S(1)}, bf16[1,32,512]{2,1,0:T(8,128)(2,1)}, u32[]{:S(2)}) copy-start(bf16[1,32,512]{2,1,0:T(8,128)(2,1)} %param.16) | copy-start | bytes 98308
  80.0 43.0 %copy-start.3 = (f32[512]{0:T(512)S(1)}, f32[512]{0:T(512)}, u32[]{:S(2)}) copy-start(f32[512]{0:T(512)} %param.18) | copy-start | bytes 6148
  92.0 20.3 %all-to-all-start = ((f32[8,32,512]{2,1,0:T(8,128)}), f32[8,32,512]{2,1,0:T(8,128)}, u32[]{:S(2)}, u32[]{:S(2)}) async-start(f32[8,32,512]{2,1,0:T(8,128)} %reshape.126), calls=%async_computation | async-start | bytes 1048576 | tf_op jit(solution)/shard_map/all_to_all | solution.py:112
  97.9 60.5 %all-reduce.2.cloned.1.call-start = ((), (), s32[]{:S(2)}) async-start(), calls=%async_computation.3 | async-start | bytes 131072 | tf_op jit(solution)/shard_map/psum | solution.py:128
Sparse Core Ops, SparseCore 0:
  125.4 32.9 all-reduce.1
where the time goes:
time: 167 us
  blocking collectives  48.8 us (29%)
  waiting for transfers between devices  38.9 us (23%)
  matrix products  21.1 us (13%)
  local copies, waits for them, and re-layouts  16.1 us (10%)
  starting transfers between devices  14.8 us (9%)
  between operations  14.2 us (9%)
  other arithmetic  12.7 us (8%)
    psum x1, waiting for transfers between devices, on_device(): mlp_total = lax.psum(mlp_part, 'tm')  33.1 us
    all_gather x1, blocking collectives, on_device(): every_query = lax.all_gather(own_queries, 'region', axis=0, tiled=True)  32.6 us
    all_gather x3, blocking collectives, joined(): everything = jax.tree.map(lambda part: lax.all_gather(part, axis), x)  16.2 us
    dot_general x1, matrix products, partials(): jnp.einsum('hqk,khd->qhd', weights.astype(jnp.bfloat16), value_heads, pre...  9.39 us
    unnamed x12, local copies, waits for them, and re-layouts  7.23 us
    all_to_all x1, starting transfers between devices, on_device(): lax.all_to_all(numerators, 'region', split_axis=0, concat_axis=0, tiled=T...  5.93 us
    all_to_all x1, waiting for transfers between devices, on_device(): lax.all_to_all(denominators, 'region', split_axis=0, concat_axis=0, tiled...  5.75 us
    all_to_all x1, starting transfers between devices, on_device(): lax.all_to_all(denominators, 'region', split_axis=0, concat_axis=0, tiled...  5.52 us
  transfers between devices with their start and end apart: 4, of which 2 were waited for; matrix products, arithmetic and copies ran while one was open for 10% of the time, Pallas kernels for 0%

commit v1 on v0

v1 whole, which is shorter than its diff:
```python
import functools

import jax
import jax.numpy as jnp
from jax import lax
from jax.experimental import pallas as pl
from jax.experimental.pallas import tpu as pltpu
from jax.sharding import PartitionSpec as P

H = 8
BLK = 256
NEG = -1e30
TILE = 8
LANES = 128
F32 = jnp.float32
BF16 = jnp.bfloat16
MESH = pl.DeviceIdType.MESH


def layer_norm(values, gain):
    average = jnp.mean(values, axis=-1, keepdims=True)
    centered = values - average
    variance = jnp.mean(centered * centered, axis=-1, keepdims=True)
    return centered * lax.rsqrt(variance + 1e-05) * gain


def columns_of(table, first, heads, lane, head_size):
    spread = jnp.broadcast_to(table[:, first : first + 1], lane.shape)
    for h in range(1, heads):
        column = table[:, first + h : first + h + 1]
        spread = jnp.where(lane >= h * head_size, column, spread)
    return spread


def turned(tiles):
    short = -len(tiles) * TILE % LANES
    if short:
        tiles = tiles + [jnp.zeros((short, tiles[0].shape[1]), F32)]
    return jnp.concatenate(tiles, axis=0).T


def kernel(
    R, T, chunk, q_block, k_block,
    counts, visible, lat, lat_gain, mlp_gain,
    obs_h, wkv_h, wq_h, wout_h, wup_h, wdn_h,
    out,
    obs, wkv, wq, wout, wup, wdn,
    lat_all, keys, values, queries, scores,
    snum, saux, gnum, gaux,
    snum2, saux2, gnum2, gaux2,
    att_own, att_all, part_own, part_all,
    load_sem, obs_sem, lat_s, lat_r,
    n1_s, n1_r, a1_s, a1_r, n2_s, n2_r, a2_s, a2_r,
    att_s, att_r, part_s, part_r,
):
    me = lax.axis_index("region")
    t = lax.axis_index("tm")
    N, D = obs.shape
    LR = lat.shape[1]
    rows = R * LR
    DH = D // H
    G = D // T
    HG = G // DH

    def region_peer(d):
        return lax.rem(me + d, R)

    def tm_peer(d):
        return lax.rem(t + d, T)

    loads = [
        pltpu.make_async_copy(src, dst, load_sem.at[i])
        for i, (src, dst) in enumerate(
            [(wkv_h, wkv), (wq_h, wq), (wout_h, wout), (wup_h, wup), (wdn_h, wdn)]
        )
    ]

    def obs_load(c):
        at = pl.ds(pl.multiple_of(c * chunk, chunk), chunk)
        return pltpu.make_async_copy(obs_h.at[0, 0, at, :], obs.at[at, :], obs_sem.at[c])

    loads[0].start()
    for c in range(N // chunk):
        obs_load(c).start()
    for load in loads[1:]:
        load.start()

    barrier = pltpu.get_barrier_semaphore()
    for d in range(1, R):
        pl.semaphore_signal(barrier, inc=1, device_id=(region_peer(d), t), device_id_type=MESH)
    for d in range(1, T):
        pl.semaphore_signal(barrier, inc=1, device_id=(me, tm_peer(d)), device_id_type=MESH)
    pl.semaphore_wait(barrier, R + T - 2)

    def lat_copy(d):
        return pltpu.make_async_remote_copy(
            lat.at[0], lat_all.at[me], lat_s.at[d], lat_r.at[d],
            device_id=(region_peer(d), t), device_id_type=MESH,
        )

    for d in range(1, R):
        lat_copy(d).start()
    lat_all[me] = lat[0]

    loads[0].wait()

    def project(c, carry):
        obs_load(c).wait()
        at = pl.ds(pl.multiple_of(c * chunk, chunk), chunk)
        kv = jnp.dot(obs[at, :], wkv[...], preferred_element_type=F32).astype(BF16)
        for g in range(T):
            keys[g, at, :] = kv[:, g * G : (g + 1) * G]
            values[g, at, :] = kv[:, D + g * G : D + (g + 1) * G]
        return carry

    lax.fori_loop(0, N // chunk, project, 0)

    for load in loads[1:]:
        load.wait()
    for d in range(1, R):
        lat_copy(d).wait_recv()
    normed = layer_norm(lat_all[...].astype(F32).reshape(rows, D), lat_gain[...]).astype(BF16)
    every = jnp.dot(normed, wq[...], preferred_element_type=F32).astype(BF16).astype(F32)
    every = (every * DH ** (-0.5)).astype(BF16)
    for g in range(T):
        queries[g] = every[:, g * G : (g + 1) * G]

    live_rows = counts[0, 0] * BLK
    lane = lax.broadcasted_iota(jnp.int32, (q_block, G), 1)
    aux_lane = lax.broadcasted_iota(jnp.int32, (q_block, LANES), 1)
    head_mask = [
        ((lane >= h * DH) & (lane < (h + 1) * DH)).astype(F32) for h in range(HG)
    ]
    k_lane = lax.broadcasted_iota(jnp.int32, (1, k_block), 1)

    def num_copy(j):
        return pltpu.make_async_remote_copy(
            snum.at[j], gnum.at[j], n1_s.at[j], n1_r.at[j],
            device_id=(me, tm_peer(j + 1)), device_id_type=MESH,
        )

    def aux_copy(j):
        return pltpu.make_async_remote_copy(
            saux.at[j], gaux.at[j], a1_s.at[j], a1_r.at[j],
            device_id=(me, tm_peer(j + 1)), device_id_type=MESH,
        )

    def lanes_reduced(x, op):
        total = x[:, :LANES]
        for i in range(1, k_block // LANES):
            total = op(total, x[:, i * LANES : (i + 1) * LANES])
        return total

    def attend(j, carry):
        g = tm_peer(j + 1)
        for b in range(rows // q_block):
            at = pl.ds(b * q_block, q_block)
            asked = queries[g, at, :].astype(F32)
            asked = jnp.concatenate([asked * mask for mask in head_mask], axis=0).astype(BF16)
            top = None
            for i in range(N // k_block):
                s = lax.dot_general(
                    asked, keys[g, pl.ds(i * k_block, k_block), :],
                    (((1,), (1,)), ((), ())), preferred_element_type=F32,
                )
                s = s + jnp.where(k_lane + i * k_block < live_rows, 0.0, NEG)
                scores[i] = s
                most = lanes_reduced(s, jnp.maximum)
                top = most if top is None else jnp.maximum(top, most)
            peak = jnp.max(top, axis=-1, keepdims=True)
            den = None
            acc = None
            for i in range(N // k_block):
                w = jnp.exp(scores[i] - peak)
                part = lanes_reduced(w, jnp.add)
                den = part if den is None else den + part
                num = jnp.dot(
                    w.astype(BF16), values[g, pl.ds(i * k_block, k_block), :],
                    preferred_element_type=F32,
                )
                acc = num if acc is None else acc + num
            den = jnp.sum(den, axis=-1, keepdims=True)
            num = acc[:q_block]
            aux = jnp.zeros((q_block, LANES), F32)
            for h in range(HG):
                rows_h = slice(h * q_block, (h + 1) * q_block)
                if h:
                    num = jnp.where(lane >= h * DH, acc[rows_h], num)
                aux = jnp.where(aux_lane == h, peak[rows_h], aux)
                aux = jnp.where(aux_lane == TILE + h, den[rows_h], aux)
            snum[j, at, :] = num.astype(BF16)
            saux[j, :, at] = aux.T[: 2 * TILE]

        @pl.when(j < T - 1)
        def _():
            num_copy(j).start()
            aux_copy(j).start()

        return carry

    lax.fori_loop(0, T, attend, 0)

    for j in range(T - 1):
        aux_copy(j).wait_recv()
    parts = [gaux[j] for j in range(T - 1)] + [saux[T - 1]]
    peaks = [part[:TILE] for part in parts]
    dens = [part[TILE:] for part in parts]
    highest = functools.reduce(jnp.maximum, peaks)
    factors = [jnp.exp(peak - highest) for peak in peaks]
    den = functools.reduce(jnp.add, [f * x for f, x in zip(factors, dens)])
    table = turned(factors)
    lane_all = lax.broadcasted_iota(jnp.int32, (rows, G), 1)
    num = snum[T - 1].astype(F32) * columns_of(table, (T - 1) * TILE, HG, lane_all, DH)
    for j in range(T - 1):
        num_copy(j).wait_recv()
        num += gnum[j].astype(F32) * columns_of(table, j * TILE, HG, lane_all, DH)
    snum2[...] = num.astype(BF16).reshape(R, LR, G)
    for r in range(R):
        seen = ((visible[r, me] > 0) | (me == r)).astype(F32)
        shift = (rows - r * LR) % rows
        peak_r = (pltpu.roll(highest, shift, 1) if shift else highest)[:, :LANES]
        den_r = (pltpu.roll(den, shift, 1) if shift else den)[:, :LANES]
        saux2[r, :TILE, :] = peak_r * seen + (1.0 - seen) * NEG
        saux2[r, TILE:, :] = den_r

    def num2_copy(d):
        return pltpu.make_async_remote_copy(
            snum2.at[region_peer(d)], gnum2.at[d], n2_s.at[d], n2_r.at[d],
            device_id=(region_peer(d), t), device_id_type=MESH,
        )

    def aux2_copy(d):
        return pltpu.make_async_remote_copy(
            saux2.at[region_peer(d)], gaux2.at[d], a2_s.at[d], a2_r.at[d],
            device_id=(region_peer(d), t), device_id_type=MESH,
        )

    for d in range(1, R):
        num2_copy(d).start()
        aux2_copy(d).start()
    for d in range(1, R):
        aux2_copy(d).wait_recv()
    parts = [saux2[me]] + [gaux2[d] for d in range(1, R)]
    peaks = [part[:TILE] for part in parts]
    highest = functools.reduce(jnp.maximum, peaks)
    factors = [jnp.exp(peak - highest) for peak in peaks]
    den = functools.reduce(jnp.add, [f * x[TILE:] for f, x in zip(factors, parts)])
    table = turned(factors + [den])[:LR]
    lane_own = lax.broadcasted_iota(jnp.int32, (LR, G), 1)
    num = snum2[me].astype(F32) * columns_of(table, 0, HG, lane_own, DH)
    for d in range(1, R):
        num2_copy(d).wait_recv()
        num += gnum2[d].astype(F32) * columns_of(table, d * TILE, HG, lane_own, DH)
    attended = (num / columns_of(table, R * TILE, HG, lane_own, DH)).astype(BF16)
    att_own[...] = attended
    att_all[t] = attended

    def att_copy(d):
        return pltpu.make_async_remote_copy(
            att_own, att_all.at[t], att_s.at[d], att_r.at[d],
            device_id=(me, tm_peer(d)), device_id_type=MESH,
        )

    for d in range(1, T):
        att_copy(d).start()
    for d in range(1, T):
        att_copy(d).wait_recv()

    residual = lat[0].astype(F32)
    residual += functools.reduce(
        jnp.add,
        [
            jnp.dot(att_all[g], wout[g * G : (g + 1) * G, :], preferred_element_type=F32)
            for g in range(T)
        ],
    )
    normed2 = layer_norm(residual, mlp_gain[...]).astype(BF16)
    hidden = jax.nn.gelu(
        jnp.dot(normed2, wup[...], preferred_element_type=F32), approximate=True
    ).astype(BF16)
    part = jnp.dot(hidden, wdn[...], preferred_element_type=F32).astype(BF16)
    part_own[...] = part
    part_all[t] = part

    def part_copy(d):
        return pltpu.make_async_remote_copy(
            part_own, part_all.at[t], part_s.at[d], part_r.at[d],
            device_id=(me, tm_peer(d)), device_id_type=MESH,
        )

    for d in range(1, T):
        part_copy(d).start()
    for d in range(1, T):
        part_copy(d).wait_recv()
    total = functools.reduce(jnp.add, [part_all[g].astype(F32) for g in range(T)])
    out[0] = (residual + total).astype(BF16)

    for d in range(1, R):
        lat_copy(d).wait_send()
        num2_copy(d).wait_send()
        aux2_copy(d).wait_send()
    for d in range(1, T):
        num_copy(d - 1).wait_send()
        aux_copy(d - 1).wait_send()
        att_copy(d).wait_send()
        part_copy(d).wait_send()


def on_device(
    R, T, observations, counts, visible, latents, lat_gain, mlp_gain,
    w_query, w_keyval, w_out, w_up, w_down,
):
    N, D = observations.shape[2:]
    LR = latents.shape[1]
    rows = R * LR
    G = D // T
    HG = G // (D // H)
    chunk = min(N, 512)
    q_block = min(rows, 256)
    k_block = min(N, 256)
    vmem = pl.BlockSpec(memory_space=pltpu.VMEM)
    smem = pl.BlockSpec(memory_space=pltpu.SMEM)
    any_space = pl.BlockSpec(memory_space=pl.ANY)
    dma = pltpu.SemaphoreType.DMA
    return pl.pallas_call(
        functools.partial(kernel, R, T, chunk, q_block, k_block),
        out_shape=jax.ShapeDtypeStruct((1, LR, D), BF16),
        in_specs=[smem, smem, vmem, vmem, vmem] + [any_space] * 6,
        out_specs=vmem,
        scratch_shapes=[
            pltpu.VMEM((N, D), BF16),
            pltpu.VMEM(w_keyval.shape, BF16),
            pltpu.VMEM(w_query.shape, BF16),
            pltpu.VMEM(w_out.shape, BF16),
            pltpu.VMEM(w_up.shape, BF16),
            pltpu.VMEM(w_down.shape, BF16),
            pltpu.VMEM((R, LR, D), BF16),
            pltpu.VMEM((T, N, G), BF16),
            pltpu.VMEM((T, N, G), BF16),
            pltpu.VMEM((T, rows, G), BF16),
            pltpu.VMEM((N // k_block, HG * q_block, k_block), F32),
            pltpu.VMEM((T, rows, G), BF16),
            pltpu.VMEM((T, 2 * TILE, rows), F32),
            pltpu.VMEM((T, rows, G), BF16),
            pltpu.VMEM((T, 2 * TILE, rows), F32),
            pltpu.VMEM((R, LR, G), BF16),
            pltpu.VMEM((R, 2 * TILE, LANES), F32),
            pltpu.VMEM((R, LR, G), BF16),
            pltpu.VMEM((R, 2 * TILE, LANES), F32),
            pltpu.VMEM((LR, G), BF16),
            pltpu.VMEM((T, LR, G), BF16),
            pltpu.VMEM((LR, D), BF16),
            pltpu.VMEM((T, LR, D), BF16),
            dma((5,)), dma((N // chunk,)), dma((R,)), dma((R,)),
            dma((T,)), dma((T,)), dma((T,)), dma((T,)),
            dma((R,)), dma((R,)), dma((R,)), dma((R,)),
            dma((T,)), dma((T,)), dma((T,)), dma((T,)),
        ],
        compiler_params=pltpu.CompilerParams(collective_id=0, has_side_effects=True),
    )(
        counts, visible, latents, lat_gain.reshape(1, D), mlp_gain.reshape(1, D),
        observations, w_keyval, w_query, w_out, w_up, w_down,
    )


def solution(mesh):
    placed = (
        P("region", "tm", None, None),
        P("region", "tm"),
        P(),
        P("region", None, None),
        P(),
        P(),
        P(),
        P(),
        P(),
        P(None, "tm"),
        P("tm", None),
    )
    return jax.shard_map(
        functools.partial(on_device, mesh.shape["region"], mesh.shape["tm"]),
        mesh=mesh, in_specs=placed, out_specs=P("region", None, None), check_vma=False,
    )
```

time: 167 us -> 42.2 us (0.25)
  blocking collectives: 48.8 us -> 0 us
  Pallas kernels: 0 us -> 39.9 us
  waiting for transfers between devices: 38.9 us -> 0 us
  matrix products: 21.1 us -> 0 us
  starting transfers between devices: 14.8 us -> 0 us
  local copies, waits for them, and re-layouts: 16.1 us -> 1.38 us
  between operations: 14.2 us -> 0.66 us
  other arithmetic: 12.7 us -> 0 us
    all_gather x4 -> x0, blocking collectives: 48.8 us -> none  [the longest x1 32.6 us: on_device(): every_query = lax.all_gather(own_queries, 'region', axis=0, tiled=True)]
    pallas_call x0 -> x1, Pallas kernels: none -> 39.9 us  [on_device(): pl.pallas_call(functools.partial(kernel, R, T, chunk, q_block, k_block),...]
    psum x1 -> x0, waiting for transfers between devices: 33.1 us -> none  [on_device(): mlp_total = lax.psum(mlp_part, 'tm')]
    dot_general x6 -> x0, matrix products: 21.1 us -> none  [the longest x1 9.39 us: partials(): jnp.einsum('hqk,khd->qhd', weights.astype(jnp.bfloat16), value_heads, pre...]
    all_to_all x3 -> x0, starting transfers between devices: 14.8 us -> none  [the longest x1 5.93 us: on_device(): lax.all_to_all(numerators, 'region', split_axis=0, concat_axis=0, tiled=T...]
    reduce_sum x6 -> x0, other arithmetic: 8.27 us -> none  [the longest x1 4.97 us: partials(): denominator = jnp.sum(weights, axis=-1)]
    unnamed x12 -> x1, local copies, waits for them, and re-layouts: 7.23 us -> 1.38 us
    all_to_all x3 -> x0, waiting for transfers between devices: 5.76 us -> none  [the longest x1 5.75 us: on_device(): lax.all_to_all(denominators, 'region', split_axis=0, concat_axis=0, tiled...]
  transfers between devices with their start and end apart: 4 -> 0, of which waited for: 2 -> 0; matrix products, arithmetic and copies ran while one was open for 10% -> 0% of each run, Pallas kernels for 0% -> 0%
where the time goes in v1:
time: 42.2 us; the launch traced here: 41.9 us
  Pallas kernels  39.9 us (95%)
  local copies, waits for them, and re-layouts  1.38 us (3%)
  between operations  0.66 us (2%)
    pallas_call x1, Pallas kernels, on_device(): pl.pallas_call(functools.partial(kernel, R, T, chunk, q_block, k_block),...  39.9 us
    unnamed x1, local copies, waits for them, and re-layouts  1.38 us

profile of v1, /device:TPU:0, one launch (start us, length us, event | category | flops | bytes accessed | tf_op | source)
XLA Modules:
  0.0 41.9 jit_solution(9151704954377590540)
XLA Ops:
  0.7 39.9 %shard_map.109 = bf16[1,32,512]{2,1,0:T(8,128)(2,1)} custom-call(s32[1,1]{1,0:T(1,128)S(6)} %copy.13.counts, s32[8,8]{1,0:T(8,128)} %visible.1, bf16[1,32,512]{2,1,0:T(8,128)(2,1)} %lat.1, f32[1,512]{1,0:T(1,128)} %bitcast.2, f32[1,512]{1,0:T(1,128)} %bitcast.3, bf16[1,1,2048,512]{3,2,1,0:T(8,128)(2,1)} %obs_h.1, bf16[512,1024]{1,0:T(8,128)(2,1)} %wkv_h.1, ...), custom_call_target="tpu_custom_call" | custom-call | tf_op jit(solution)/shard_map/pallas_call | solution.py:325
  40.6 1.4 %copy.14 = bf16[1,32,512]{2,1,0:T(8,128)(2,1)} copy(bf16[1,32,512]{2,1,0:T(8,128)(2,1)} %shard_map.109) | data formatting | bytes 65536

commit v2 on v1

--- a/solution.py
+++ b/solution.py
@@ -11,6 +11,7 @@
 BLK = 256
 NEG = -1e30
 TILE = 8
+HALF = TILE // 2
 LANES = 128
 F32 = jnp.float32
 BF16 = jnp.bfloat16
@@ -32,6 +33,15 @@
     return spread
 
 
+def joined(parts):
+    highest = functools.reduce(jnp.maximum, parts)
+    factors = [jnp.exp(part - highest) for part in parts]
+    den = functools.reduce(
+        jnp.add, [pltpu.roll(f, HALF, 0) * part for f, part in zip(factors, parts)]
+    )
+    return highest, factors, den
+
+
 def turned(tiles):
     short = -len(tiles) * TILE % LANES
     if short:
@@ -40,16 +50,16 @@
 
 
 def kernel(
-    R, T, chunk, q_block, k_block,
+    R, T, chunk, q_block, row_slice,
     counts, visible, lat, lat_gain, mlp_gain,
     obs_h, wkv_h, wq_h, wout_h, wup_h, wdn_h,
     out,
     obs, wkv, wq, wout, wup, wdn,
-    lat_all, keys, values, queries, scores,
+    lat_all, keys, values, queries, scores, weights,
     snum, saux, gnum, gaux,
     snum2, saux2, gnum2, gaux2,
     att_own, att_all, part_own, part_all,
-    load_sem, obs_sem, lat_s, lat_r,
+    load_sem, obs_sem, lat_s, lat_r, mate_s, mate_r,
     n1_s, n1_r, a1_s, a1_r, n2_s, n2_r, a2_s, a2_r,
     att_s, att_r, part_s, part_r,
 ):
@@ -92,10 +102,22 @@
         pl.semaphore_signal(barrier, inc=1, device_id=(me, tm_peer(d)), device_id_type=MESH)
     pl.semaphore_wait(barrier, R + T - 2)
 
+    halves = 2 if T % 2 == 0 else 1
+    half = LR // halves
+    mate = t + 1 - 2 * lax.rem(t, 2)
+    mine = pl.ds(pl.multiple_of(lax.rem(t, halves) * half, half), half)
+
     def lat_copy(d):
         return pltpu.make_async_remote_copy(
-            lat.at[0], lat_all.at[me], lat_s.at[d], lat_r.at[d],
+            lat.at[0, mine, :], lat_all.at[me, mine, :], lat_s.at[d], lat_r.at[d],
             device_id=(region_peer(d), t), device_id_type=MESH,
+        )
+
+    def mate_copy(d):
+        source = region_peer(R - d)
+        return pltpu.make_async_remote_copy(
+            lat_all.at[source, mine, :], lat_all.at[source, mine, :], mate_s.at[d], mate_r.at[d],
+            device_id=(me, mate), device_id_type=MESH,
         )
 
     for d in range(1, R):
@@ -115,10 +137,14 @@
 
     lax.fori_loop(0, N // chunk, project, 0)
 
-    for load in loads[1:]:
-        load.wait()
+    loads[1].wait()
     for d in range(1, R):
         lat_copy(d).wait_recv()
+        if halves == 2:
+            mate_copy(d).start()
+    if halves == 2:
+        for d in range(1, R):
+            mate_copy(d).wait_recv()
     normed = layer_norm(lat_all[...].astype(F32).reshape(rows, D), lat_gain[...]).astype(BF16)
     every = jnp.dot(normed, wq[...], preferred_element_type=F32).astype(BF16).astype(F32)
     every = (every * DH ** (-0.5)).astype(BF16)
@@ -131,7 +157,7 @@
     head_mask = [
         ((lane >= h * DH) & (lane < (h + 1) * DH)).astype(F32) for h in range(HG)
     ]
-    k_lane = lax.broadcasted_iota(jnp.int32, (1, k_block), 1)
+    live = lax.broadcasted_iota(jnp.int32, (1, N), 1) < live_rows
 
     def num_copy(j):
         return pltpu.make_async_remote_copy(
@@ -146,40 +172,32 @@
         )
 
     def lanes_reduced(x, op):
-        total = x[:, :LANES]
-        for i in range(1, k_block // LANES):
-            total = op(total, x[:, i * LANES : (i + 1) * LANES])
-        return total
+        return functools.reduce(op, [x[:, i : i + LANES] for i in range(0, N, LANES)])
 
     def attend(j, carry):
         g = tm_peer(j + 1)
+        bias = jnp.where(live, 0.0, NEG)
         for b in range(rows // q_block):
             at = pl.ds(b * q_block, q_block)
             asked = queries[g, at, :].astype(F32)
             asked = jnp.concatenate([asked * mask for mask in head_mask], axis=0).astype(BF16)
-            top = None
-            for i in range(N // k_block):
-                s = lax.dot_general(
-                    asked, keys[g, pl.ds(i * k_block, k_block), :],
-                    (((1,), (1,)), ((), ())), preferred_element_type=F32,
-                )
-                s = s + jnp.where(k_lane + i * k_block < live_rows, 0.0, NEG)
-                scores[i] = s
-                most = lanes_reduced(s, jnp.maximum)
-                top = most if top is None else jnp.maximum(top, most)
-            peak = jnp.max(top, axis=-1, keepdims=True)
-            den = None
-            acc = None
-            for i in range(N // k_block):
-                w = jnp.exp(scores[i] - peak)
-                part = lanes_reduced(w, jnp.add)
-                den = part if den is None else den + part
-                num = jnp.dot(
-                    w.astype(BF16), values[g, pl.ds(i * k_block, k_block), :],
-                    preferred_element_type=F32,
-                )
-                acc = num if acc is None else acc + num
-            den = jnp.sum(den, axis=-1, keepdims=True)
+            scores[b] = bias + lax.dot_general(
+                asked, keys[g], (((1,), (1,)), ((), ())), preferred_element_type=F32
+            )
+        for b in range(rows // q_block):
+            at = pl.ds(b * q_block, q_block)
+            peaks = []
+            dens = []
+            for r in range(0, HG * q_block, row_slice):
+                s = scores[b, r : r + row_slice, :]
+                peak = jnp.max(lanes_reduced(s, jnp.maximum), axis=-1, keepdims=True)
+                w = jnp.exp(s - peak)
+                dens.append(jnp.sum(lanes_reduced(w, jnp.add), axis=-1, keepdims=True))
+                peaks.append(peak)
+                weights[b, r : r + row_slice, :] = w.astype(BF16)
+            acc = jnp.dot(weights[b], values[g], preferred_element_type=F32)
+            peak = jnp.concatenate(peaks, axis=0)
+            den = jnp.concatenate(dens, axis=0)
             num = acc[:q_block]
             aux = jnp.zeros((q_block, LANES), F32)
             for h in range(HG):
@@ -187,9 +205,9 @@
                 if h:
                     num = jnp.where(lane >= h * DH, acc[rows_h], num)
                 aux = jnp.where(aux_lane == h, peak[rows_h], aux)
-                aux = jnp.where(aux_lane == TILE + h, den[rows_h], aux)
+                aux = jnp.where(aux_lane == HALF + h, den[rows_h], aux)
             snum[j, at, :] = num.astype(BF16)
-            saux[j, :, at] = aux.T[: 2 * TILE]
+            saux[j, :, at] = aux.T[:TILE]
 
         @pl.when(j < T - 1)
         def _():
@@ -203,11 +221,7 @@
     for j in range(T - 1):
         aux_copy(j).wait_recv()
     parts = [gaux[j] for j in range(T - 1)] + [saux[T - 1]]
-    peaks = [part[:TILE] for part in parts]
-    dens = [part[TILE:] for part in parts]
-    highest = functools.reduce(jnp.maximum, peaks)
-    factors = [jnp.exp(peak - highest) for peak in peaks]
-    den = functools.reduce(jnp.add, [f * x for f, x in zip(factors, dens)])
+    highest, factors, den = joined(parts)
     table = turned(factors)
     lane_all = lax.broadcasted_iota(jnp.int32, (rows, G), 1)
     num = snum[T - 1].astype(F32) * columns_of(table, (T - 1) * TILE, HG, lane_all, DH)
@@ -215,13 +229,13 @@
         num_copy(j).wait_recv()
         num += gnum[j].astype(F32) * columns_of(table, j * TILE, HG, lane_all, DH)
     snum2[...] = num.astype(BF16).reshape(R, LR, G)
+    merged = jnp.where(lax.broadcasted_iota(jnp.int32, den.shape, 0) < HALF, highest, den)
+    is_peak = lax.broadcasted_iota(jnp.int32, (TILE, LANES), 0) < HALF
     for r in range(R):
         seen = ((visible[r, me] > 0) | (me == r)).astype(F32)
         shift = (rows - r * LR) % rows
-        peak_r = (pltpu.roll(highest, shift, 1) if shift else highest)[:, :LANES]
-        den_r = (pltpu.roll(den, shift, 1) if shift else den)[:, :LANES]
-        saux2[r, :TILE, :] = peak_r * seen + (1.0 - seen) * NEG
-        saux2[r, TILE:, :] = den_r
+        tile = (pltpu.roll(merged, shift, 1) if shift else merged)[:, :LANES]
+        saux2[r] = jnp.where(is_peak, tile * seen + (1.0 - seen) * NEG, tile)
 
     def num2_copy(d):
         return pltpu.make_async_remote_copy(
@@ -241,17 +255,14 @@
     for d in range(1, R):
         aux2_copy(d).wait_recv()
     parts = [saux2[me]] + [gaux2[d] for d in range(1, R)]
-    peaks = [part[:TILE] for part in parts]
-    highest = functools.reduce(jnp.maximum, peaks)
-    factors = [jnp.exp(peak - highest) for peak in peaks]
-    den = functools.reduce(jnp.add, [f * x[TILE:] for f, x in zip(factors, parts)])
+    highest, factors, den = joined(parts)
     table = turned(factors + [den])[:LR]
     lane_own = lax.broadcasted_iota(jnp.int32, (LR, G), 1)
     num = snum2[me].astype(F32) * columns_of(table, 0, HG, lane_own, DH)
     for d in range(1, R):
         num2_copy(d).wait_recv()
         num += gnum2[d].astype(F32) * columns_of(table, d * TILE, HG, lane_own, DH)
-    attended = (num / columns_of(table, R * TILE, HG, lane_own, DH)).astype(BF16)
+    attended = (num / columns_of(table, R * TILE + HALF, HG, lane_own, DH)).astype(BF16)
     att_own[...] = attended
     att_all[t] = attended
 
@@ -265,6 +276,9 @@
         att_copy(d).start()
     for d in range(1, T):
         att_copy(d).wait_recv()
+
+    for load in loads[2:]:
+        load.wait()
 
     residual = lat[0].astype(F32)
     residual += functools.reduce(
@@ -297,6 +311,8 @@
 
     for d in range(1, R):
         lat_copy(d).wait_send()
+        if halves == 2:
+            mate_copy(d).wait_send()
         num2_copy(d).wait_send()
         aux2_copy(d).wait_send()
     for d in range(1, T):
@@ -316,14 +332,14 @@
     G = D // T
     HG = G // (D // H)
     chunk = min(N, 512)
-    q_block = min(rows, 256)
-    k_block = min(N, 256)
+    q_block = min(rows, 128)
+    row_slice = min(q_block, 16)
     vmem = pl.BlockSpec(memory_space=pltpu.VMEM)
     smem = pl.BlockSpec(memory_space=pltpu.SMEM)
     any_space = pl.BlockSpec(memory_space=pl.ANY)
     dma = pltpu.SemaphoreType.DMA
     return pl.pallas_call(
-        functools.partial(kernel, R, T, chunk, q_block, k_block),
+        functools.partial(kernel, R, T, chunk, q_block, row_slice),
         out_shape=jax.ShapeDtypeStruct((1, LR, D), BF16),
         in_specs=[smem, smem, vmem, vmem, vmem] + [any_space] * 6,
         out_specs=vmem,
@@ -338,20 +354,21 @@
             pltpu.VMEM((T, N, G), BF16),
             pltpu.VMEM((T, N, G), BF16),
             pltpu.VMEM((T, rows, G), BF16),
-            pltpu.VMEM((N // k_block, HG * q_block, k_block), F32),
+            pltpu.VMEM((rows // q_block, HG * q_block, N), F32),
+            pltpu.VMEM((rows // q_block, HG * q_block, N), BF16),
             pltpu.VMEM((T, rows, G), BF16),
-            pltpu.VMEM((T, 2 * TILE, rows), F32),
+            pltpu.VMEM((T, TILE, rows), F32),
             pltpu.VMEM((T, rows, G), BF16),
-            pltpu.VMEM((T, 2 * TILE, rows), F32),
+            pltpu.VMEM((T, TILE, rows), F32),
             pltpu.VMEM((R, LR, G), BF16),
-            pltpu.VMEM((R, 2 * TILE, LANES), F32),
+            pltpu.VMEM((R, TILE, LANES), F32),
             pltpu.VMEM((R, LR, G), BF16),
-            pltpu.VMEM((R, 2 * TILE, LANES), F32),
+            pltpu.VMEM((R, TILE, LANES), F32),
             pltpu.VMEM((LR, G), BF16),
             pltpu.VMEM((T, LR, G), BF16),
             pltpu.VMEM((LR, D), BF16),
             pltpu.VMEM((T, LR, D), BF16),
-            dma((5,)), dma((N // chunk,)), dma((R,)), dma((R,)),
+            dma((5,)), dma((N // chunk,)), dma((R,)), dma((R,)), dma((R,)), dma((R,)),
             dma((T,)), dma((T,)), dma((T,)), dma((T,)),
             dma((R,)), dma((R,)), dma((R,)), dma((R,)),
             dma((T,)), dma((T,)), dma((T,)), dma((T,)),

time: 42.2 us -> 35.8 us (0.85)
  Pallas kernels: 39.9 us -> 33.6 us
    pallas_call x1, Pallas kernels: 39.9 us -> 33.6 us  [on_device(): pl.pallas_call(functools.partial(kernel, R, T, chunk, q_block, row_slice)...]
where the time goes in v2:
time: 35.8 us; the launch traced here: 35.6 us
  Pallas kernels  33.6 us (94%)
  local copies, waits for them, and re-layouts  1.38 us (4%)
  between operations  0.66 us (2%)
    pallas_call x1, Pallas kernels, on_device(): pl.pallas_call(functools.partial(kernel, R, T, chunk, q_block, row_slice)...  33.6 us
    unnamed x1, local copies, waits for them, and re-layouts  1.38 us

profile of v2, /device:TPU:0, one launch (start us, length us, event | category | flops | bytes accessed | tf_op | source)
XLA Modules:
  0.0 35.6 jit_solution(14461523417529803502)
XLA Ops:
  0.7 33.6 %shard_map.109 = bf16[1,32,512]{2,1,0:T(8,128)(2,1)} custom-call(s32[1,1]{1,0:T(1,128)S(6)} %copy.13.counts, s32[8,8]{1,0:T(8,128)} %visible.1, bf16[1,32,512]{2,1,0:T(8,128)(2,1)} %lat.1, f32[1,512]{1,0:T(1,128)} %bitcast.2, f32[1,512]{1,0:T(1,128)} %bitcast.3, bf16[1,1,2048,512]{3,2,1,0:T(8,128)(2,1)} %obs_h.1, bf16[512,1024]{1,0:T(8,128)(2,1)} %wkv_h.1, ...), custom_call_target="tpu_custom_call" | custom-call | tf_op jit(solution)/shard_map/pallas_call | solution.py:341
  34.2 1.4 %copy.14 = bf16[1,32,512]{2,1,0:T(8,128)(2,1)} copy(bf16[1,32,512]{2,1,0:T(8,128)(2,1)} %shard_map.109) | data formatting | bytes 65536
